TPU v7x, 32 devices: a whole 2x2x4 slice. The times are simulated.
32 devices in a mesh: pat: 2 (over y), slab: 4 (over z), phase: 2 (over x), enc: 2 (over core).
Axes of the slice: x: 2, y: 2, z: 4, core: 2. Of those that a mesh axis runs over, the one named last changes fastest.
Arguments:
- kspace_data: bfloat16 [4, 2, 4, 96, 64, 192], P('pat', 'phase', 'enc', 'slab'), parts along dimension 0, may hold values from -6 to 6
- coil_maps: bfloat16 [4, 24, 4, 64, 192], P('pat', None, None, 'slab'), parts along dimension 0, may hold values from -1 to 1
- sampling: int32 [2, 4, 128, 192], P('phase', 'enc', 'pat'), parts along dimension 2, may hold values 0 or 1
Outputs:
- image_estimate: float32 [4, 2, 4, 4, 64, 192], P('pat', 'phase', 'enc', None, 'slab'), parts along dimension 0
- residual: float32 [4, 2, 4, 96, 64, 192], P('pat', 'phase', 'enc', 'slab'), parts along dimension 0
There are 2 independent parts, one for each index of `pat`. A program takes and returns all parts, laid end to end along the dimension named above; each array names one. Nothing has to cross between parts.
All inputs are finite; a program needn't handle non-finite values. No bound on the sum of `sampling` on one device may be relied on, other than what follows from the above.
Results may differ from a plain program's by a relative error of at most 0.0046.
Values may be sent and summed in bfloat16 or wider, within the bound.
A program may use at most 64 MiB of HBM per device.

v0:
```python
import math
import jax
import jax.numpy as jnp
from jax import lax
from jax.sharding import PartitionSpec as P

ITERS = 2
tv_weight = 0.15
smoothing = 0.6


def with_halo(value, sides, width):
    for axis, dim in sides:
        size, length = (lax.axis_size(axis), value.shape[dim])
        up = [(i, (i + 1) % size) for i in range(size)]
        down = [(j, i) for i, j in up]
        last = lax.slice_in_dim(value, length - width, length, axis=dim)
        first = lax.slice_in_dim(value, 0, width, axis=dim)
        before = lax.ppermute(last, axis, up)
        after = lax.ppermute(first, axis, down)
        value = jnp.concatenate([before, value, after], axis=dim)
    return value


def dft_table(length, direction):
    counter = jnp.arange(length, dtype=jnp.int32)
    product = counter[:, None] * counter[None, :] % length
    angle = product.astype(jnp.float32) * (2.0 * math.pi / length)
    factor = 1.0 / math.sqrt(length)
    return (
        (jnp.cos(angle) * factor).astype(jnp.bfloat16),
        (direction * jnp.sin(angle) * factor).astype(jnp.bfloat16),
    )


def along_rows(real_part, imag_part, table):
    cosine, sine = table
    real_out = jnp.matmul(real_part, cosine, preferred_element_type=jnp.float32) - jnp.matmul(
        imag_part, sine, preferred_element_type=jnp.float32
    )
    imag_out = jnp.matmul(real_part, sine, preferred_element_type=jnp.float32) + jnp.matmul(
        imag_part, cosine, preferred_element_type=jnp.float32
    )
    return (real_out, imag_out)


def along_depth(real_part, imag_part, table):
    cosine, sine = table
    real_out = jnp.einsum(
        "...zy,zw->...wy", real_part, cosine, preferred_element_type=jnp.float32
    ) - jnp.einsum("...zy,zw->...wy", imag_part, sine, preferred_element_type=jnp.float32)
    imag_out = jnp.einsum(
        "...zy,zw->...wy", real_part, sine, preferred_element_type=jnp.float32
    ) + jnp.einsum("...zy,zw->...wy", imag_part, cosine, preferred_element_type=jnp.float32)
    return (real_out, imag_out)


def coil_product(coil_real, coil_imag, real_in, imag_in, column_fwd):
    prod_real = (coil_real * real_in - coil_imag * imag_in).astype(jnp.bfloat16)
    prod_imag = (coil_real * imag_in + coil_imag * real_in).astype(jnp.bfloat16)
    mid_real, mid_imag = along_rows(prod_real, prod_imag, column_fwd)
    return jnp.stack([mid_real, mid_imag]).astype(jnp.bfloat16)


def body(kspace_data, coil_maps, sampling):
    phases = kspace_data.shape[1]
    encodings = kspace_data.shape[2]
    coils = coil_maps.shape[1]
    readout = coil_maps.shape[2]
    zdepth = coil_maps.shape[3]
    lines = coil_maps.shape[4]
    slices = kspace_data.shape[4]
    column_fwd = dft_table(lines, -1.0)
    depth_fwd = dft_table(slices, -1.0)
    column_inv = dft_table(lines, 1.0)
    depth_inv = dft_table(slices, 1.0)
    coil_real = coil_maps[0].astype(jnp.float32)
    coil_imag = coil_maps[1].astype(jnp.float32)
    sampled = sampling.astype(jnp.float32)[None, :, :, None]
    residual = -(kspace_data.astype(jnp.float32) * sampled)
    image_estimate = jnp.zeros((2, phases, encodings, readout, zdepth, lines), jnp.float32)
    row_count = kspace_data.shape[3]
    coil_rows = lax.all_to_all(
        coil_maps.reshape(2, coils * readout, zdepth, lines),
        "slab",
        split_axis=1,
        concat_axis=2,
        tiled=True,
    )
    row_columns = (
        lax.axis_index("slab") * row_count + jnp.arange(row_count, dtype=jnp.int32)
    ) % readout
    for iteration in range(ITERS):
        low = residual.astype(jnp.bfloat16)
        inv_real, inv_imag = along_depth(low[0], low[1], depth_inv)
        partial_rows = jnp.stack([inv_real, inv_imag]).astype(jnp.bfloat16)
        portion = lax.all_to_all(partial_rows, "slab", split_axis=4, concat_axis=3, tiled=True)
        shaped = portion.reshape(
            2,
            portion.shape[1],
            portion.shape[2],
            coils,
            readout,
            portion.shape[4],
            portion.shape[5],
        )
        fine_real, fine_imag = along_rows(shaped[0], shaped[1], column_inv)
        grad_real = jnp.sum(coil_real * fine_real + coil_imag * fine_imag, axis=2)
        grad_imag = jnp.sum(coil_real * fine_imag - coil_imag * fine_real, axis=2)
        adjoint = jnp.stack([grad_real, grad_imag])
        padded = with_halo(image_estimate, (("phase", 1),), 1)
        difference = padded[:, 1:] - padded[:, :-1]
        modulus = difference[0] * difference[0] + difference[1] * difference[1]
        weights = difference / jnp.sqrt(modulus + smoothing * smoothing)[None]
        gradient = adjoint + tv_weight * (weights[:, :-1] - weights[:, 1:])
        grad_local = jnp.sum(gradient * gradient)
        grad_sq = lax.psum(grad_local, ("slab", "phase", "enc"))
        low_grad = gradient.astype(jnp.bfloat16)
        picked = jnp.take(
            lax.all_gather(low_grad, "slab", axis=4, tiled=True), row_columns, axis=3
        ).astype(jnp.float32)
        local_coils = coil_rows.astype(jnp.float32)
        mid = coil_product(local_coils[0], local_coils[1], picked[0], picked[1], column_fwd)
        out_real, out_imag = along_depth(mid[0], mid[1], depth_fwd)
        spectrum = jnp.stack([out_real, out_imag])
        spectrum = spectrum * sampled
        spec_local = jnp.sum(spectrum * spectrum)
        spec_sq = lax.psum(spec_local, ("slab", "phase", "enc"))
        alpha = grad_sq / (spec_sq + 4.0 * tv_weight / smoothing * grad_sq + 1e-06)
        image_estimate = image_estimate - alpha * gradient
        residual = residual - alpha * spectrum
    return (image_estimate, residual)


def solution(mesh):
    in_specs = (
        P("pat", "phase", "enc", "slab", None, None),
        P("pat", None, None, "slab", None),
        P("phase", "enc", "pat", None),
    )
    out_specs = (
        P("pat", "phase", "enc", None, "slab", None),
        P("pat", "phase", "enc", "slab", None, None),
    )
    return jax.shard_map(body, mesh=mesh, in_specs=in_specs, out_specs=out_specs, check_vma=False)
```

profile of v0, /device:TPU:0, one launch (start us, length us, event | category | flops | bytes accessed | tf_op | source)
XLA Modules:
  0.0 373.4 jit_solution(6726968447215893808)
XLA Ops:
  0.7 2.9 copy.52
  3.6 6.3 %all-to-all-start.1 = ((bf16[2,96,16,192]{3,2,0,1:T(8,128)(2,1)}), bf16[2,96,16,192]{3,2,0,1:T(8,128)(2,1)}, u32[]{:S(2)}, u32[]{:S(2)}) async-start(bf16[2,96,16,192]{3,2,0,1:T(8,128)(2,1)} %bitcast.243), calls=%async_computation.1 | async-start | bytes 3145728 | tf_op jit(solution)/shard_map/all_to_all | solution.py:83
  9.9 0.9 fusion
  11.5 0.7 fusion.4
  12.9 0.7 fusion.5
  14.2 3.4 copy.50
  17.7 29.3 %all-to-all-done.1 = bf16[2,96,16,192]{3,2,0,1:T(8,128)(2,1)} async-done(((bf16[2,96,16,192]{3,2,0,1:T(8,128)(2,1)}), bf16[2,96,16,192]{3,2,0,1:T(8,128)(2,1)}, u32[]{:S(2)}, u32[]{:S(2)}) %all-to-all-start.1) | async-done | bytes 1179680 | tf_op jit(solution)/shard_map/all_to_all | solution.py:83
  47.0 4.8 %all-to-all-start = ((bf16[2,1,2,24,64,192]{5,3,2,1,0,4:T(8,128)(2,1)}), bf16[2,1,2,24,64,192]{5,3,2,1,0,4:T(8,128)(2,1)}, u32[]{:S(2)}, u32[]{:S(2)}) async-start(bf16[2,1,2,24,64,192]{5,3,2,1,0,4:T(8,128)(2,1)} %copy.50), calls=%async_computation | async-start | bytes 6291456 | tf_op jit(solution)/shard_map/all_to_all | solution.py:97
  51.8 0.7 broadcast_in_dim.8
  52.5 1.5 collective-permute-start
  54.6 1.8 bitcast_convert_fusion.1
  56.4 5.5 %collective-permute-done = f32[2,1,2,4,16,192]{5,4,3,2,0,1:T(8,128)S(1)} collective-permute-done((f32[2,1,2,4,16,192]{5,4,3,2,0,1:T(8,128)}, f32[2,1,2,4,16,192]{5,4,3,2,0,1:T(8,128)S(1)}, u32[]{:S(2)}, u32[]{:S(2)}) %collective-permute-start) | collective-permute-done | bytes 196640 | tf_op jit(solution)/shard_map/ppermute | solution.py:20
  61.9 3.9 %collective-permute-done.1 = f32[2,1,2,4,16,192]{5,4,3,2,0,1:T(8,128)} collective-permute-done((f32[2,1,2,4,16,192]{5,4,3,2,0,1:T(8,128)}, f32[2,1,2,4,16,192]{5,4,3,2,0,1:T(8,128)}, u32[]{:S(2)}, u32[]{:S(2)}) %collective-permute-start.1) | collective-permute-done | bytes 196640 | tf_op jit(solution)/shard_map/ppermute | solution.py:19
  65.8 1.1 fusion.30
  66.9 1.8 fusion.24
  68.7 1.9 convert_bitcast_fusion
  71.0 1.4 copy.53
  72.4 1.3 copy.55
  73.7 48.4 %all-to-all-done = bf16[2,1,2,24,64,192]{5,3,2,1,0,4:T(8,128)(2,1)} async-done(((bf16[2,1,2,24,64,192]{5,3,2,1,0,4:T(8,128)(2,1)}), bf16[2,1,2,24,64,192]{5,3,2,1,0,4:T(8,128)(2,1)}, u32[]{:S(2)}, u32[]{:S(2)}) %all-to-all-start) | async-done | bytes 2359328 | tf_op jit(solution)/shard_map/all_to_all | solution.py:97
  122.1 3.7 copy.96
  126.0 1.3 fusion.57
  127.2 1.3 fusion.66
  128.6 1.4 convolution_subtract_fusion.1
  129.9 2.4 add_reduce_fusion.1
  132.4 16.1 %all_gather.6 = bf16[2,1,2,4,64,192]{5,4,3,2,0,1:T(8,128)(2,1)S(1)} all-gather(bf16[2,1,2,4,16,192]{5,4,3,2,0,1:T(8,128)(2,1)S(1)} %get-tuple-element.19), channel_id=1, replica_groups=mesh['pat'=2,'slab'=4,'phase'=2,'enc'=2] {'slab'}, dimensions={4}, use_global_device_ids=true | all-gather | bytes 491520 | tf_op jit(solution)/shard_map/all_gather | solution.py:120
  148.5 2.5 gather_fusion
  151.1 2.5 fusion.2
  153.9 1.3 add_convert_fusion.4
  155.2 1.3 fusion.20
  156.5 1.3 fusion.22
  157.8 1.3 subtract_convert_fusion.3
  160.4 1.3 add_convert_fusion.3
  163.2 2.2 multiply_reduce_fusion.1
  166.1 30.6 %all-reduce.3 = (f32[]{:T(128)}, f32[]{:T(128)}) all-reduce(f32[]{:T(128)} %multiply_reduce_fusion.3, f32[]{:T(128)} %multiply_reduce_fusion.1), channel_id=1, replica_groups=mesh['pat'=2,'slab'=4,'phase'=2,'enc'=2] {'slab','phase','enc'}, use_global_device_ids=true, to_apply=%region_3.4 | all-reduce | flops 2 | bytes 16 | tf_op jit(solution)/shard_map/psum | solution.py:117
  198.6 3.6 fusion.3
  203.5 0.7 fusion.6
  204.3 0.7 fusion.7
  205.6 3.4 copy.60
  209.1 4.6 %all-to-all-start.2 = ((bf16[2,1,2,24,64,192]{5,3,2,1,0,4:T(8,128)(2,1)}), bf16[2,1,2,24,64,192]{5,3,2,1,0,4:T(8,128)(2,1)}, u32[]{:S(2)}, u32[]{:S(2)}) async-start(bf16[2,1,2,24,64,192]{5,3,2,1,0,4:T(8,128)(2,1)} %copy.60), calls=%async_computation.2 | async-start | bytes 6291456 | tf_op jit(solution)/shard_map/all_to_all | solution.py:97
  213.8 2.0 collective-permute-start.3
  215.8 7.2 %collective-permute-done.2 = f32[2,1,2,4,16,192]{5,4,3,2,0,1:T(8,128)S(1)} collective-permute-done((f32[2,1,2,4,16,192]{5,4,3,2,0,1:T(8,128)S(1)}, f32[2,1,2,4,16,192]{5,4,3,2,0,1:T(8,128)S(1)}, u32[]{:S(2)}, u32[]{:S(2)}) %collective-permute-start.2) | collective-permute-done | bytes 196640 | tf_op jit(solution)/shard_map/ppermute | solution.py:20
  223.0 4.5 %collective-permute-done.3 = f32[2,1,2,4,16,192]{5,4,3,2,0,1:T(8,128)S(1)} collective-permute-done((f32[2,1,2,4,16,192]{5,4,3,2,0,1:T(8,128)S(1)}, f32[2,1,2,4,16,192]{5,4,3,2,0,1:T(8,128)S(1)}, u32[]{:S(2)}, u32[]{:S(2)}) %collective-permute-start.3) | collective-permute-done | bytes 196640 | tf_op jit(solution)/shard_map/ppermute | solution.py:19
  227.7 0.9 broadcast_divide_fusion
  228.6 56.1 %all-to-all-done.2 = bf16[2,1,2,24,64,192]{5,3,2,1,0,4:T(8,128)(2,1)} async-done(((bf16[2,1,2,24,64,192]{5,3,2,1,0,4:T(8,128)(2,1)}), bf16[2,1,2,24,64,192]{5,3,2,1,0,4:T(8,128)(2,1)}, u32[]{:S(2)}, u32[]{:S(2)}) %all-to-all-start.2) | async-done | bytes 2359328 | tf_op jit(solution)/shard_map/all_to_all | solution.py:97
  284.7 3.7 copy.95
  288.7 1.3 fusion.54
  290.0 1.3 fusion.63
  291.3 1.3 convolution_subtract_fusion
  293.2 2.4 add_reduce_fusion
  295.6 0.8 fusion.244
  296.4 17.0 %all_gather.7 = bf16[2,1,2,4,64,192]{5,4,3,2,0,1:T(8,128)(2,1)} all-gather(bf16[2,1,2,4,16,192]{5,4,3,2,0,1:T(8,128)(2,1)S(1)} %get-tuple-element.17), channel_id=1, replica_groups=mesh['pat'=2,'slab'=4,'phase'=2,'enc'=2] {'slab'}, dimensions={4}, use_global_device_ids=true | all-gather | bytes 491520 | tf_op jit(solution)/shard_map/all_gather | solution.py:120
  313.4 3.6 gather_fusion.1
  317.0 2.6 fusion.1
  319.8 1.3 add_convert_fusion.1
  321.1 1.3 fusion.14
  322.4 1.3 fusion.16
  323.7 1.3 subtract_convert_fusion
  326.3 1.3 add_convert_fusion
  328.3 0.7 add_bitcast_fusion
  329.0 1.0 copy-done.6
  330.0 2.2 multiply_reduce_fusion
  332.9 30.1 %all-reduce.2 = (f32[]{:T(128)}, f32[]{:T(128)}) all-reduce(f32[]{:T(128)} %multiply_reduce_fusion.2, f32[]{:T(128)} %multiply_reduce_fusion), channel_id=1, replica_groups=mesh['pat'=2,'slab'=4,'phase'=2,'enc'=2] {'slab','phase','enc'}, use_global_device_ids=true, to_apply=%region_9.11 | all-reduce | flops 2 | bytes 16 | tf_op jit(solution)/shard_map/psum | solution.py:117
  365.0 7.4 %multiply_subtract_fusion = f32[2,1,2,24,64,192]{5,4,3,2,1,0:T(8,128)} fusion(f32[1,1,2,24,64,192]{5,4,3,2,1,0:T(8,128)} %copy-done.7, f32[1,1,2,24,64,192]{5,4,3,2,1,0:T(8,128)} %copy-done.6, f32[]{:T(128)S(6)} %div.33, f32[2,64,192]{2,1,0:T(8,128)S(1)} %convert_bitcast_fusion.1, f32[1,1,2,24,64,192]{5,4,3,2,1,0:T(8,128)} %copy-done, ...), kind=kLoop, calls=%fused_computation.4 | loop fusion | flops 12976128 | bytes 16613384 | tf_op jit(solution)/shard_map/sub | solution.py:131
  372.4 0.7 subtract_bitcast_fusion.2
  (61 shorter events, 13.0 us)
Async XLA Ops:
  0.6 9.3 %copy-start.16 = (s32[1,2,64,192]{3,2,1,0:T(8,128)S(1)}, s32[1,2,64,192]{3,2,1,0:T(8,128)}, u32[]{:S(2)}) copy-start(s32[1,2,64,192]{3,2,1,0:T(8,128)} %param.7) | copy-start | bytes 294916
  0.6 9.3 %copy-start.5 = (bf16[2,1,2,24,64,192]{5,4,3,2,1,0:T(8,128)(2,1)S(1)}, bf16[2,1,2,24,64,192]{5,4,3,2,1,0:T(8,128)(2,1)}, u32[]{:S(2)}) copy-start(bf16[2,1,2,24,64,192]{5,4,3,2,1,0:T(8,128)(2,1)} %param.5) | copy-start | bytes 7077892
  3.6 43.4 %all-to-all-start.1 = ((bf16[2,96,16,192]{3,2,0,1:T(8,128)(2,1)}), bf16[2,96,16,192]{3,2,0,1:T(8,128)(2,1)}, u32[]{:S(2)}, u32[]{:S(2)}) async-start(bf16[2,96,16,192]{3,2,0,1:T(8,128)(2,1)} %bitcast.243), calls=%async_computation.1 | async-start | bytes 3145728 | tf_op jit(solution)/shard_map/all_to_all | solution.py:83
  47.0 75.1 %all-to-all-start = ((bf16[2,1,2,24,64,192]{5,3,2,1,0,4:T(8,128)(2,1)}), bf16[2,1,2,24,64,192]{5,3,2,1,0,4:T(8,128)(2,1)}, u32[]{:S(2)}, u32[]{:S(2)}) async-start(bf16[2,1,2,24,64,192]{5,3,2,1,0,4:T(8,128)(2,1)} %copy.50), calls=%async_computation | async-start | bytes 6291456 | tf_op jit(solution)/shard_map/all_to_all | solution.py:97
  52.5 9.4 %collective-permute-start = (f32[2,1,2,4,16,192]{5,4,3,2,0,1:T(8,128)}, f32[2,1,2,4,16,192]{5,4,3,2,0,1:T(8,128)S(1)}, u32[]{:S(2)}, u32[]{:S(2)}) collective-permute-start(f32[2,1,2,4,16,192]{5,4,3,2,0,1:T(8,128)} %broadcast_in_dim.8), channel_id=1, source_target_pairs={{2,0},{0,2},{3,1},{1,3},{6,4},{4,6},{7,5},{5,7},{10,8},{8,10},{11,... | collective-permute-start | bytes 589832 | tf_op jit(solution)/shard_map/ppermute | solution.py:20
  54.0 11.8 %collective-permute-start.1 = (f32[2,1,2,4,16,192]{5,4,3,2,0,1:T(8,128)}, f32[2,1,2,4,16,192]{5,4,3,2,0,1:T(8,128)}, u32[]{:S(2)}, u32[]{:S(2)}) collective-permute-start(f32[2,1,2,4,16,192]{5,4,3,2,0,1:T(8,128)} %broadcast_in_dim.8), channel_id=1, source_target_pairs={{0,2},{2,0},{1,3},{3,1},{4,6},{6,4},{5,7},{7,5},{8,10},{10,8},{9,1... | collective-permute-start | bytes 589832 | tf_op jit(solution)/shard_map/ppermute | solution.py:19
  56.4 73.5 %copy-start.1 = (f32[24,4,16,192]{3,2,1,0:T(8,128)}, f32[24,4,16,192]{3,2,1,0:T(8,128)S(1)}, u32[]{:S(2)}) copy-start(f32[24,4,16,192]{3,2,1,0:T(8,128)S(1)} %get-tuple-element.31) | copy-start | bytes 3538948
  56.4 73.5 %copy-start.3 = (f32[24,4,16,192]{3,2,1,0:T(8,128)}, f32[24,4,16,192]{3,2,1,0:T(8,128)S(1)}, u32[]{:S(2)}) copy-start(f32[24,4,16,192]{3,2,1,0:T(8,128)S(1)} %get-tuple-element.32) | copy-start | bytes 3538948
  129.9 2.4 copy-start.15
  151.1 2.5 copy-start.8
  151.1 2.8 copy-start.10
  163.2 2.2 copy-start
  209.1 75.7 %all-to-all-start.2 = ((bf16[2,1,2,24,64,192]{5,3,2,1,0,4:T(8,128)(2,1)}), bf16[2,1,2,24,64,192]{5,3,2,1,0,4:T(8,128)(2,1)}, u32[]{:S(2)}, u32[]{:S(2)}) async-start(bf16[2,1,2,24,64,192]{5,3,2,1,0,4:T(8,128)(2,1)} %copy.60), calls=%async_computation.2 | async-start | bytes 6291456 | tf_op jit(solution)/shard_map/all_to_all | solution.py:97
  213.7 9.2 %collective-permute-start.2 = (f32[2,1,2,4,16,192]{5,4,3,2,0,1:T(8,128)S(1)}, f32[2,1,2,4,16,192]{5,4,3,2,0,1:T(8,128)S(1)}, u32[]{:S(2)}, u32[]{:S(2)}) collective-permute-start(f32[2,1,2,4,16,192]{5,4,3,2,0,1:T(8,128)S(1)} %multiply_subtract_fusion.2), channel_id=1, source_target_pairs={{2,0},{0,2},{3,1},{1,3},{6,4},{4,6},{7,5},{5,7},{10,8},{8,10},{11,... | collective-permute-start | bytes 589832 | tf_op jit(solution)/shard_map/ppermute | solution.py:20
  213.8 13.7 %collective-permute-start.3 = (f32[2,1,2,4,16,192]{5,4,3,2,0,1:T(8,128)S(1)}, f32[2,1,2,4,16,192]{5,4,3,2,0,1:T(8,128)S(1)}, u32[]{:S(2)}, u32[]{:S(2)}) collective-permute-start(f32[2,1,2,4,16,192]{5,4,3,2,0,1:T(8,128)S(1)} %multiply_subtract_fusion.2), channel_id=1, source_target_pairs={{0,2},{2,0},{1,3},{3,1},{4,6},{6,4},{5,7},{7,5},{8,10},{10,8},{9,1... | collective-permute-start | bytes 589832 | tf_op jit(solution)/shard_map/ppermute | solution.py:19
  291.3 1.4 copy-start.2
  291.3 1.9 copy-start.4
  293.2 2.4 copy-start.14
  317.0 2.6 copy-start.9
  317.0 2.8 copy-start.11
  328.3 1.7 copy-start.6
  330.0 2.3 copy-start.7
  330.0 2.3 copy-start.12
  365.0 7.4 %copy-start.13 = (f32[2,1,2,4,16,192]{5,4,3,2,0,1:T(8,128)S(1)}, f32[2,1,2,4,16,192]{5,4,3,2,0,1:T(8,128)}, u32[]{:S(2)}) copy-start(f32[2,1,2,4,16,192]{5,4,3,2,0,1:T(8,128)} %get-tuple-element.18) | copy-start | bytes 589828
where the time goes:
time: 379 us; the launch traced here: 373 us
  waiting for transfers between devices  155 us (41%)
  blocking collectives  93.8 us (25%)
  other arithmetic  35.8 us (9%)
  matrix products  34.2 us (9%)
  local copies, waits for them, and re-layouts  29.6 us (8%)
  starting transfers between devices  19.9 us (5%)
  between operations  5.16 us (1%)
    all_to_all x2, waiting for transfers between devices, body(): lax.all_to_all(partial_rows, 'slab', split_axis=4, concat_axis=3, tiled=T...  105 us
    psum x2, blocking collectives, body(): grad_sq = lax.psum(grad_local, ('slab', 'phase', 'enc'))  60.7 us
    all_gather x2, blocking collectives, body(): lax.all_gather(low_grad, 'slab', axis=4, tiled=True)  33.1 us
    all_to_all x1, waiting for transfers between devices, body(): lax.all_to_all(coil_maps.reshape(2, coils * readout, zdepth, lines), 'sla...  29.3 us
    ppermute x2, waiting for transfers between devices, with_halo(): after = lax.ppermute(first, axis, down)  12.6 us
    all_to_all x2, starting transfers between devices, body(): lax.all_to_all(partial_rows, 'slab', split_axis=4, concat_axis=3, tiled=T...  9.46 us
    ppermute x2, waiting for transfers between devices, with_halo(): before = lax.ppermute(last, axis, up)  8.38 us
  transfers between devices with their start and end apart: 7, of which 7 were waited for; matrix products, arithmetic and copies ran while one was open for 5% of the time, Pallas kernels for 0%

commit v1 on v0

--- a/solution.py
+++ b/solution.py
@@ -80,12 +80,20 @@
     residual = -(kspace_data.astype(jnp.float32) * sampled)
     image_estimate = jnp.zeros((2, phases, encodings, readout, zdepth, lines), jnp.float32)
     row_count = kspace_data.shape[3]
-    coil_rows = lax.all_to_all(
-        coil_maps.reshape(2, coils * readout, zdepth, lines),
-        "slab",
-        split_axis=1,
-        concat_axis=2,
-        tiled=True,
+    coil_rows = jnp.concatenate(
+        lax.all_to_all(
+            jnp.stack(
+                jnp.split(
+                    coil_maps.reshape(2, coils * readout, zdepth, lines),
+                    lax.axis_size("slab"),
+                    axis=1,
+                )
+            ),
+            "slab",
+            0,
+            0,
+        ),
+        axis=2,
     )
     row_columns = (
         lax.axis_index("slab") * row_count + jnp.arange(row_count, dtype=jnp.int32)

time: 379 us -> 379 us (level)
  no operation moved by 1% of the time
where the time goes in v1:
time: 379 us; the launch traced here: 374 us
  waiting for transfers between devices  155 us (41%)
  blocking collectives  93.8 us (25%)
  other arithmetic  37.3 us (10%)
  matrix products  34.2 us (9%)
  local copies, waits for them, and re-layouts  28.1 us (7%)
  starting transfers between devices  20.1 us (5%)
  between operations  5.09 us (1%)
    all_to_all x2, waiting for transfers between devices, body(): lax.all_to_all(partial_rows, 'slab', split_axis=4, concat_axis=3, tiled=T...  105 us
    psum x2, blocking collectives, body(): grad_sq = lax.psum(grad_local, ('slab', 'phase', 'enc'))  60.7 us
    all_gather x2, blocking collectives, body(): lax.all_gather(low_grad, 'slab', axis=4, tiled=True)  33.2 us
    all_to_all x1, waiting for transfers between devices, body(): lax.all_to_all(jnp.stack(jnp.split(coil_maps.reshape(2, coils * readout,...  29.3 us
    ppermute x2, waiting for transfers between devices, with_halo(): after = lax.ppermute(first, axis, down)  12.6 us
    all_to_all x2, starting transfers between devices, body(): lax.all_to_all(partial_rows, 'slab', split_axis=4, concat_axis=3, tiled=T...  9.46 us
    ppermute x2, waiting for transfers between devices, with_halo(): before = lax.ppermute(last, axis, up)  8.38 us
  transfers between devices with their start and end apart: 7, of which 7 were waited for; matrix products, arithmetic and copies ran while one was open for 5% of the time, Pallas kernels for 0%

profile of v1, /device:TPU:0, one launch (start us, length us, event | category | flops | bytes accessed | tf_op | source)
XLA Modules:
  0.0 373.5 jit_solution(14623851110073757523)
XLA Ops:
  0.6 1.5 slice_bitcast_fusion.19
  2.1 1.5 pad_maximum_fusion.2
  3.7 6.5 %all-to-all-start.1 = ((bf16[4,2,24,16,192]{4,3,2,1,0:T(8,128)(2,1)}), bf16[4,2,24,16,192]{4,3,2,1,0:T(8,128)(2,1)}, u32[]{:S(2)}, u32[]{:S(2)}) async-start(bf16[4,2,24,16,192]{4,3,2,1,0:T(8,128)(2,1)} %pad_maximum_fusion.2), calls=%async_computation.1 | async-start | bytes 3145728 | tf_op jit(solution)/shard_map/all_to_all | solution.py:84
  10.2 0.9 fusion
  13.1 0.7 fusion.5
  14.4 3.4 copy.53
  17.9 29.3 %all-to-all-done.1 = bf16[4,2,24,16,192]{4,3,2,1,0:T(8,128)(2,1)} async-done(((bf16[4,2,24,16,192]{4,3,2,1,0:T(8,128)(2,1)}), bf16[4,2,24,16,192]{4,3,2,1,0:T(8,128)(2,1)}, u32[]{:S(2)}, u32[]{:S(2)}) %all-to-all-start.1) | async-done | bytes 1179680 | tf_op jit(solution)/shard_map/all_to_all | solution.py:84
  47.2 4.8 %all-to-all-start = ((bf16[2,1,2,24,64,192]{5,3,2,1,0,4:T(8,128)(2,1)}), bf16[2,1,2,24,64,192]{5,3,2,1,0,4:T(8,128)(2,1)}, u32[]{:S(2)}, u32[]{:S(2)}) async-start(bf16[2,1,2,24,64,192]{5,3,2,1,0,4:T(8,128)(2,1)} %copy.53), calls=%async_computation | async-start | bytes 6291456 | tf_op jit(solution)/shard_map/all_to_all | solution.py:105
  52.0 0.7 broadcast_in_dim.8
  52.8 1.5 collective-permute-start
  54.8 1.8 bitcast_convert_fusion.1
  56.7 5.5 %collective-permute-done = f32[2,1,2,4,16,192]{5,4,3,2,0,1:T(8,128)S(1)} collective-permute-done((f32[2,1,2,4,16,192]{5,4,3,2,0,1:T(8,128)}, f32[2,1,2,4,16,192]{5,4,3,2,0,1:T(8,128)S(1)}, u32[]{:S(2)}, u32[]{:S(2)}) %collective-permute-start) | collective-permute-done | bytes 196640 | tf_op jit(solution)/shard_map/ppermute | solution.py:20
  62.1 3.9 %collective-permute-done.1 = f32[2,1,2,4,16,192]{5,4,3,2,0,1:T(8,128)} collective-permute-done((f32[2,1,2,4,16,192]{5,4,3,2,0,1:T(8,128)}, f32[2,1,2,4,16,192]{5,4,3,2,0,1:T(8,128)}, u32[]{:S(2)}, u32[]{:S(2)}) %collective-permute-start.1) | collective-permute-done | bytes 196640 | tf_op jit(solution)/shard_map/ppermute | solution.py:19
  66.0 1.1 fusion.30
  67.1 1.8 fusion.24
  68.9 1.8 convert_bitcast_fusion
  71.1 1.4 copy.55
  72.5 1.3 copy.57
  73.8 48.5 %all-to-all-done = bf16[2,1,2,24,64,192]{5,3,2,1,0,4:T(8,128)(2,1)} async-done(((bf16[2,1,2,24,64,192]{5,3,2,1,0,4:T(8,128)(2,1)}), bf16[2,1,2,24,64,192]{5,3,2,1,0,4:T(8,128)(2,1)}, u32[]{:S(2)}, u32[]{:S(2)}) %all-to-all-start) | async-done | bytes 2359328 | tf_op jit(solution)/shard_map/all_to_all | solution.py:105
  122.3 3.7 copy.98
  126.2 1.3 fusion.57
  127.5 1.3 fusion.66
  128.8 1.4 convolution_subtract_fusion.1
  130.2 2.4 add_reduce_fusion.1
  132.7 16.1 %all_gather.6 = bf16[2,1,2,4,64,192]{5,4,3,2,0,1:T(8,128)(2,1)S(1)} all-gather(bf16[2,1,2,4,16,192]{5,4,3,2,0,1:T(8,128)(2,1)S(1)} %get-tuple-element.19), channel_id=1, replica_groups=mesh['pat'=2,'slab'=4,'phase'=2,'enc'=2] {'slab'}, dimensions={4}, use_global_device_ids=true | all-gather | bytes 491520 | tf_op jit(solution)/shard_map/all_gather | solution.py:128
  148.8 2.5 gather_fusion
  151.3 2.5 fusion.2
  154.1 1.3 add_convert_fusion.4
  155.4 1.3 fusion.20
  156.7 1.3 fusion.22
  158.0 1.3 subtract_convert_fusion.3
  160.7 1.3 add_convert_fusion.3
  162.7 0.7 add_bitcast_fusion.1
  163.4 2.2 multiply_reduce_fusion.1
  166.3 30.6 %all-reduce.3 = (f32[]{:T(128)}, f32[]{:T(128)}) all-reduce(f32[]{:T(128)} %multiply_reduce_fusion.3, f32[]{:T(128)} %multiply_reduce_fusion.1), channel_id=1, replica_groups=mesh['pat'=2,'slab'=4,'phase'=2,'enc'=2] {'slab','phase','enc'}, use_global_device_ids=true, to_apply=%region_3.4 | all-reduce | flops 2 | bytes 16 | tf_op jit(solution)/shard_map/psum | solution.py:125
  198.8 3.6 fusion.3
  203.8 0.7 fusion.6
  204.5 0.7 fusion.7
  205.9 3.4 copy.62
  209.3 4.7 %all-to-all-start.2 = ((bf16[2,1,2,24,64,192]{5,3,2,1,0,4:T(8,128)(2,1)}), bf16[2,1,2,24,64,192]{5,3,2,1,0,4:T(8,128)(2,1)}, u32[]{:S(2)}, u32[]{:S(2)}) async-start(bf16[2,1,2,24,64,192]{5,3,2,1,0,4:T(8,128)(2,1)} %copy.62), calls=%async_computation.2 | async-start | bytes 6291456 | tf_op jit(solution)/shard_map/all_to_all | solution.py:105
  214.1 2.0 collective-permute-start.3
  216.1 7.2 %collective-permute-done.2 = f32[2,1,2,4,16,192]{5,4,3,2,0,1:T(8,128)S(1)} collective-permute-done((f32[2,1,2,4,16,192]{5,4,3,2,0,1:T(8,128)S(1)}, f32[2,1,2,4,16,192]{5,4,3,2,0,1:T(8,128)S(1)}, u32[]{:S(2)}, u32[]{:S(2)}) %collective-permute-start.2) | collective-permute-done | bytes 196640 | tf_op jit(solution)/shard_map/ppermute | solution.py:20
  223.2 4.5 %collective-permute-done.3 = f32[2,1,2,4,16,192]{5,4,3,2,0,1:T(8,128)S(1)} collective-permute-done((f32[2,1,2,4,16,192]{5,4,3,2,0,1:T(8,128)S(1)}, f32[2,1,2,4,16,192]{5,4,3,2,0,1:T(8,128)S(1)}, u32[]{:S(2)}, u32[]{:S(2)}) %collective-permute-start.3) | collective-permute-done | bytes 196640 | tf_op jit(solution)/shard_map/ppermute | solution.py:19
  227.9 0.9 broadcast_divide_fusion
  228.8 56.1 %all-to-all-done.2 = bf16[2,1,2,24,64,192]{5,3,2,1,0,4:T(8,128)(2,1)} async-done(((bf16[2,1,2,24,64,192]{5,3,2,1,0,4:T(8,128)(2,1)}), bf16[2,1,2,24,64,192]{5,3,2,1,0,4:T(8,128)(2,1)}, u32[]{:S(2)}, u32[]{:S(2)}) %all-to-all-start.2) | async-done | bytes 2359328 | tf_op jit(solution)/shard_map/all_to_all | solution.py:105
  285.0 3.7 copy.97
  288.9 1.3 fusion.54
  290.2 1.3 fusion.63
  291.6 1.4 convolution_subtract_fusion
  293.4 2.4 add_reduce_fusion
  295.8 0.8 fusion.244
  296.6 17.1 %all_gather.7 = bf16[2,1,2,4,64,192]{5,4,3,2,0,1:T(8,128)(2,1)} all-gather(bf16[2,1,2,4,16,192]{5,4,3,2,0,1:T(8,128)(2,1)S(1)} %get-tuple-element.17), channel_id=1, replica_groups=mesh['pat'=2,'slab'=4,'phase'=2,'enc'=2] {'slab'}, dimensions={4}, use_global_device_ids=true | all-gather | bytes 491520 | tf_op jit(solution)/shard_map/all_gather | solution.py:128
  313.7 3.6 gather_fusion.1
  317.2 2.6 fusion.1
  320.1 1.3 add_convert_fusion.1
  321.3 1.3 fusion.14
  322.6 1.3 fusion.16
  323.9 1.3 subtract_convert_fusion
  326.6 1.3 add_convert_fusion
  329.3 1.0 copy-done.6
  330.3 2.2 multiply_reduce_fusion
  333.2 30.1 %all-reduce.2 = (f32[]{:T(128)}, f32[]{:T(128)}) all-reduce(f32[]{:T(128)} %multiply_reduce_fusion.2, f32[]{:T(128)} %multiply_reduce_fusion), channel_id=1, replica_groups=mesh['pat'=2,'slab'=4,'phase'=2,'enc'=2] {'slab','phase','enc'}, use_global_device_ids=true, to_apply=%region_9.11 | all-reduce | flops 2 | bytes 16 | tf_op jit(solution)/shard_map/psum | solution.py:125
  365.2 7.4 %multiply_subtract_fusion = f32[2,1,2,24,64,192]{5,4,3,2,1,0:T(8,128)} fusion(f32[1,1,2,24,64,192]{5,4,3,2,1,0:T(8,128)} %copy-done.7, f32[1,1,2,24,64,192]{5,4,3,2,1,0:T(8,128)} %copy-done.6, f32[]{:T(128)S(6)} %div.33, f32[2,64,192]{2,1,0:T(8,128)S(1)} %convert_bitcast_fusion.1, f32[1,1,2,24,64,192]{5,4,3,2,1,0:T(8,128)} %copy-done, ...), kind=kLoop, calls=%fused_computation.4 | loop fusion | flops 12976128 | bytes 16613384 | tf_op jit(solution)/shard_map/sub | solution.py:139
  372.6 0.7 subtract_bitcast_fusion.2
  (62 shorter events, 13.5 us)
Async XLA Ops:
  2.1 8.0 %copy-start.16 = (s32[1,2,64,192]{3,2,1,0:T(8,128)S(1)}, s32[1,2,64,192]{3,2,1,0:T(8,128)}, u32[]{:S(2)}) copy-start(s32[1,2,64,192]{3,2,1,0:T(8,128)} %param.7) | copy-start | bytes 294916
  2.1 8.1 %copy-start.5 = (bf16[2,1,2,24,64,192]{5,4,3,2,1,0:T(8,128)(2,1)S(1)}, bf16[2,1,2,24,64,192]{5,4,3,2,1,0:T(8,128)(2,1)}, u32[]{:S(2)}) copy-start(bf16[2,1,2,24,64,192]{5,4,3,2,1,0:T(8,128)(2,1)} %param.5) | copy-start | bytes 7077892
  3.7 43.5 %all-to-all-start.1 = ((bf16[4,2,24,16,192]{4,3,2,1,0:T(8,128)(2,1)}), bf16[4,2,24,16,192]{4,3,2,1,0:T(8,128)(2,1)}, u32[]{:S(2)}, u32[]{:S(2)}) async-start(bf16[4,2,24,16,192]{4,3,2,1,0:T(8,128)(2,1)} %pad_maximum_fusion.2), calls=%async_computation.1 | async-start | bytes 3145728 | tf_op jit(solution)/shard_map/all_to_all | solution.py:84
  47.2 75.1 %all-to-all-start = ((bf16[2,1,2,24,64,192]{5,3,2,1,0,4:T(8,128)(2,1)}), bf16[2,1,2,24,64,192]{5,3,2,1,0,4:T(8,128)(2,1)}, u32[]{:S(2)}, u32[]{:S(2)}) async-start(bf16[2,1,2,24,64,192]{5,3,2,1,0,4:T(8,128)(2,1)} %copy.53), calls=%async_computation | async-start | bytes 6291456 | tf_op jit(solution)/shard_map/all_to_all | solution.py:105
  52.8 9.4 %collective-permute-start = (f32[2,1,2,4,16,192]{5,4,3,2,0,1:T(8,128)}, f32[2,1,2,4,16,192]{5,4,3,2,0,1:T(8,128)S(1)}, u32[]{:S(2)}, u32[]{:S(2)}) collective-permute-start(f32[2,1,2,4,16,192]{5,4,3,2,0,1:T(8,128)} %broadcast_in_dim.8), channel_id=1, source_target_pairs={{2,0},{0,2},{3,1},{1,3},{6,4},{4,6},{7,5},{5,7},{10,8},{8,10},{11,... | collective-permute-start | bytes 589832 | tf_op jit(solution)/shard_map/ppermute | solution.py:20
  54.3 11.8 %collective-permute-start.1 = (f32[2,1,2,4,16,192]{5,4,3,2,0,1:T(8,128)}, f32[2,1,2,4,16,192]{5,4,3,2,0,1:T(8,128)}, u32[]{:S(2)}, u32[]{:S(2)}) collective-permute-start(f32[2,1,2,4,16,192]{5,4,3,2,0,1:T(8,128)} %broadcast_in_dim.8), channel_id=1, source_target_pairs={{0,2},{2,0},{1,3},{3,1},{4,6},{6,4},{5,7},{7,5},{8,10},{10,8},{9,1... | collective-permute-start | bytes 589832 | tf_op jit(solution)/shard_map/ppermute | solution.py:19
  56.6 73.6 %copy-start.1 = (f32[24,4,16,192]{3,2,1,0:T(8,128)}, f32[24,4,16,192]{3,2,1,0:T(8,128)S(1)}, u32[]{:S(2)}) copy-start(f32[24,4,16,192]{3,2,1,0:T(8,128)S(1)} %get-tuple-element.35) | copy-start | bytes 3538948
  56.6 73.6 %copy-start.3 = (f32[24,4,16,192]{3,2,1,0:T(8,128)}, f32[24,4,16,192]{3,2,1,0:T(8,128)S(1)}, u32[]{:S(2)}) copy-start(f32[24,4,16,192]{3,2,1,0:T(8,128)S(1)} %get-tuple-element.36) | copy-start | bytes 3538948
  130.2 2.4 copy-start.15
  151.3 2.5 copy-start.8
  151.3 2.8 copy-start.10
  163.4 2.2 copy-start
  209.3 75.7 %all-to-all-start.2 = ((bf16[2,1,2,24,64,192]{5,3,2,1,0,4:T(8,128)(2,1)}), bf16[2,1,2,24,64,192]{5,3,2,1,0,4:T(8,128)(2,1)}, u32[]{:S(2)}, u32[]{:S(2)}) async-start(bf16[2,1,2,24,64,192]{5,3,2,1,0,4:T(8,128)(2,1)} %copy.62), calls=%async_computation.2 | async-start | bytes 6291456 | tf_op jit(solution)/shard_map/all_to_all | solution.py:105
  214.0 9.2 %collective-permute-start.2 = (f32[2,1,2,4,16,192]{5,4,3,2,0,1:T(8,128)S(1)}, f32[2,1,2,4,16,192]{5,4,3,2,0,1:T(8,128)S(1)}, u32[]{:S(2)}, u32[]{:S(2)}) collective-permute-start(f32[2,1,2,4,16,192]{5,4,3,2,0,1:T(8,128)S(1)} %multiply_subtract_fusion.2), channel_id=1, source_target_pairs={{2,0},{0,2},{3,1},{1,3},{6,4},{4,6},{7,5},{5,7},{10,8},{8,10},{11,... | collective-permute-start | bytes 589832 | tf_op jit(solution)/shard_map/ppermute | solution.py:20
  214.1 13.7 %collective-permute-start.3 = (f32[2,1,2,4,16,192]{5,4,3,2,0,1:T(8,128)S(1)}, f32[2,1,2,4,16,192]{5,4,3,2,0,1:T(8,128)S(1)}, u32[]{:S(2)}, u32[]{:S(2)}) collective-permute-start(f32[2,1,2,4,16,192]{5,4,3,2,0,1:T(8,128)S(1)} %multiply_subtract_fusion.2), channel_id=1, source_target_pairs={{0,2},{2,0},{1,3},{3,1},{4,6},{6,4},{5,7},{7,5},{8,10},{10,8},{9,1... | collective-permute-start | bytes 589832 | tf_op jit(solution)/shard_map/ppermute | solution.py:19
  291.5 1.4 copy-start.2
  291.6 1.9 copy-start.4
  293.4 2.4 copy-start.14
  317.2 2.6 copy-start.9
  317.2 2.8 copy-start.11
  328.6 1.7 copy-start.6
  330.3 2.2 copy-start.7
  330.3 2.2 copy-start.12
  365.2 7.4 %copy-start.13 = (f32[2,1,2,4,16,192]{5,4,3,2,0,1:T(8,128)S(1)}, f32[2,1,2,4,16,192]{5,4,3,2,0,1:T(8,128)}, u32[]{:S(2)}) copy-start(f32[2,1,2,4,16,192]{5,4,3,2,0,1:T(8,128)} %get-tuple-element.18) | copy-start | bytes 589828
